TPU v7x, 32 devices: a whole 2x2x4 slice. The times are simulated.
32 devices in a mesh: gx: 4 (over y, core), gy: 2 (over x), gz: 4 (over z).
Axes of the slice: x: 2, y: 2, z: 4, core: 2. Of those that a mesh axis runs over, the one named last changes fastest.
Arguments:
- source: float32 [256, 128, 128], P('gx', 'gy', 'gz'), may hold values from -6 to 6
- green: float32 [512, 256, 256], P(None, ('gx', 'gz'), 'gy'), may hold values from 0.05 to 2, as said below
Outputs:
- potential: float32 [256, 128, 128], P('gx', 'gy', 'gz')
Inputs may be any that keep to these rules, and one draw needn't show every extreme that they name: `green`: greenfull is even: greenfull[k] equals greenfull at (-k1 mod 512, -k2 mod 256, -k3 mod 256).
All inputs are finite; a program needn't handle non-finite values.
Results may differ from a plain program's by a relative error of at most 0.00007.
Values sent between devices are 32-bit elements; how exact they have to be, the bound alone decides.
A program may use at most 128 MiB of HBM per device.

v0:
```python
import functools
import math

import jax
import jax.numpy as jnp
import ml_dtypes
import numpy as np
from jax import lax
from jax.experimental import pallas as pl
from jax.experimental.pallas import tpu as pltpu
from jax.sharding import PartitionSpec as P

LANES = 128
PARTS = 2
CHUNKS = 2
VMEM_BYTES = 48 * 1024 * 1024


def np_halves(table):
    high = table.astype(np.float32).astype(ml_dtypes.bfloat16)
    low = (table - high.astype(np.float64)).astype(np.float32).astype(ml_dtypes.bfloat16)
    return np.stack([high, low])


def split(value):
    high = value.astype(jnp.bfloat16)
    return high, (value - high.astype(jnp.float32)).astype(jnp.bfloat16)


def mm(left, right):
    return jnp.dot(left, right, preferred_element_type=jnp.float32)


def table_left(high, low, value):
    v_high, v_low = split(value)
    both = mm(high, jnp.concatenate([v_high, v_low], axis=1))
    width = value.shape[1]
    return both[:, :width] + (both[:, width:] + mm(low, v_high))


def table_right(value, high, low):
    v_high, v_low = split(value)
    return mm(v_high, high) + (mm(v_low, high) + mm(v_high, low))


def block_swap(pieces, width):
    count = len(pieces)
    group = lax.broadcasted_iota(jnp.int32, pieces[0].shape, 1) // width
    out = []
    for c in range(count):
        total = None
        for g in range(count):
            moved = pieces[g]
            shift = (g - c) * width % LANES
            if shift:
                moved = pltpu.roll(moved, shift, 1)
            total = moved if total is None else jnp.where(group == g, moved, total)
        out.append(total)
    return out


def y_tables(length_y, blocks, units, scale):
    cells = np.arange(length_y // 2)
    freq = np.arange(length_y // 2)
    angle = 2.0 * np.pi * (np.outer(freq, cells) % length_y) / length_y
    sign = 1.0 - 2.0 * (cells % 2)
    real, imag = np.cos(angle), -np.sin(angle)
    imag[0] = sign
    weight = np.where(freq == 0, 1.0, 2.0)[:, None] * (scale / length_y)
    both = np.stack([real, imag], axis=1)
    back = both * weight[:, None]

    def ordered(table):
        table = table.reshape(blocks, 2, PARTS, units // PARTS, 2, -1)
        return table.transpose(1, 2, 0, 3, 4, 5).reshape(2, length_y // 2, -1)

    forward = np.swapaxes(np_halves(ordered(both)), 0, 1)
    backward = np.swapaxes(np_halves(np.swapaxes(ordered(back), 1, 2)), 0, 1)
    return forward, backward


def x_table(length_x, group, rows):
    freqs = np.arange(length_x // 4)
    place = np.arange(length_x // 4)
    block, rest = place // (group * rows), place % (group * rows)
    cells = block * group * rows + rest % rows * group + rest // rows
    out = []
    for member in range(4):
        freq = 4 * freqs + member
        angle = 2.0 * np.pi * (np.outer(freq, cells) % length_x) / length_x
        out.append(np.concatenate([np.cos(angle), np.sin(angle)], 1))
    return np_halves(np.stack(out))


def z_table(length_z, parts):
    place = np.arange(length_z)
    unit, member = place // 2, place % 2
    freq = np.where(unit == 0, member * (length_z // 2), np.where(member == 0, unit, length_z - unit))
    cells = np.arange(length_z // 2)
    rows = []
    for freqs in np.split(freq, parts):
        angle = 2.0 * np.pi * (np.outer(cells, freqs) % length_z) / length_z
        rows.append(np.concatenate([np.cos(angle), -np.sin(angle)], 1))
    return np_halves(np.stack(rows))


def expand(source, out, back):
    size = source.shape[2]
    for part in range(2):
        for m in range(source.shape[1]):
            c = source[part, m, :, :size].astype(jnp.float32)
            s = source[part, m, :, size:].astype(jnp.float32)
            full = jnp.concatenate(
                [jnp.concatenate([c, s], axis=1), jnp.concatenate([-s, c], axis=1)], axis=0
            )
            out[part, m] = full.astype(jnp.bfloat16)
            back[part, m] = full.T.astype(jnp.bfloat16)


def whole_kernel(
    size_gx, size_gz, units,
    source_hbm, green_hbm, y_hbm, yback_hbm, x_hbm, z_hbm, out_ref,
    source, green, y_tab, y_back, x_half, z_half, x_tab, x_back, z_tab, z_back,
    raw_own, raw_other, green_own, green_sent, green_other, nyquist, distant,
    f_sent, f_got, b_sent, b_got, lines, spectrum, part_own, part_sent, part_other,
    local_sem, send_sem, raw_sem, green_sem, f_sem, b_sem, part_sem,
):
    gx, gy, gz = lax.axis_index("gx"), lax.axis_index("gy"), lax.axis_index("gz")
    blocks = size_gx * size_gz
    block = gx * size_gz + gz
    group = size_gz
    width = LANES // group
    rows = raw_own.shape[1]
    count_y = raw_own.shape[2]
    each = units // PARTS
    piece = 2 * each * rows
    share = green_own.shape[3]
    quarter = green_own.shape[2]
    half_x = 2 * quarter
    positions = 4 * units
    partner = {"gy": 1 - gy}
    lower = gy == 0
    packed = block + gy == 0

    def remote(source_at, target_at, sent, got, device):
        return pltpu.make_async_remote_copy(
            source_at, target_at, send_sem.at[sent], got,
            device_id=device, device_id_type=pl.DeviceIdType.MESH,
        )

    def plane_device(step):
        target = lax.rem(block + step, blocks)
        return target, {"gx": target // size_gz, "gz": lax.rem(target, size_gz)}

    def span(part, chunk, at):
        start = ((part * CHUNKS + chunk) * blocks + at) * piece
        return pl.ds(pl.multiple_of(start, 8), piece)

    def send_plane(sent_ref, got_ref, which, sems, part, chunk):
        def body(step, _):
            target, device = plane_device(step)
            remote(
                sent_ref.at[span(part, chunk, target), :],
                got_ref.at[span(part, chunk, block), :],
                which, sems.at[part, chunk], device,
            ).start()
            return 0

        lax.fori_loop(1, blocks, body, 0)
        got_ref[span(part, chunk, block), :] = sent_ref[span(part, chunk, block), :]

    def wait_plane(got_ref, which, sems, part, chunk):
        everything = got_ref.at[pl.ds(0, (blocks - 1) * piece), :]
        remote(everything, everything, which, sems.at[part, chunk], partner).wait_recv()

    step_x = rows * group
    copies = [
        pltpu.make_async_copy(
            source_hbm.at[pl.ds(c * step_x, step_x)], source.at[pl.ds(c * step_x, step_x)], local_sem.at[c]
        )
        for c in range(CHUNKS)
    ]
    copies += [
        pltpu.make_async_copy(green_hbm, green, local_sem.at[CHUNKS]),
        pltpu.make_async_copy(x_hbm, x_half, local_sem.at[CHUNKS + 1]),
        pltpu.make_async_copy(z_hbm, z_half, local_sem.at[CHUNKS + 2]),
        pltpu.make_async_copy(y_hbm.at[gy], y_tab, local_sem.at[CHUNKS + 3]),
        pltpu.make_async_copy(yback_hbm.at[gy], y_back, local_sem.at[CHUNKS + 4]),
    ]
    for copy in copies:
        copy.start()

    barrier = pltpu.get_barrier_semaphore()

    def greet(step, _):
        _, device = plane_device(step)
        pl.semaphore_signal(barrier, inc=1, device_id=device, device_id_type=pl.DeviceIdType.MESH)
        return 0

    pl.semaphore_signal(barrier, inc=1, device_id=partner, device_id_type=pl.DeviceIdType.MESH)
    lax.fori_loop(1, blocks, greet, 0)

    for c in range(CHUNKS):
        copies[c].wait()
        for a in range(rows):
            at = (c * rows + a) * group
            raw_own[c, a] = jnp.concatenate([source[at + b] for b in range(group)], axis=0).T

    pl.semaphore_wait(barrier, blocks)

    for c in range(CHUNKS):
        for a in range(rows):
            remote(raw_own.at[c, a], raw_other.at[c, a], 0, raw_sem.at[c, a], partner).start()

    copies[CHUNKS].wait()

    def extract(step, _):
        u, m = step // 4, lax.rem(step, 4)
        for half, out in ((gy, green_own), (1 - gy, green_sent)):
            at = m * positions + 2 * (half * units + u)
            out[u, m] = green[pl.ds(at, quarter, stride=4 * positions), :]
        return 0

    lax.fori_loop(0, 4 * units, extract, 0)
    for m in range(4):
        nyquist[m] = green[pl.ds(m * positions + 1, quarter, stride=4 * positions), :]
    copies[CHUNKS + 1].wait()
    copies[CHUNKS + 2].wait()
    expand(x_half, x_tab, x_back)
    expand(z_half, z_tab, z_back)
    copies[CHUNKS + 3].wait()
    copies[CHUNKS + 4].wait()

    def transform(c):
        def body(a, _):
            remote(raw_own.at[c, a], raw_other.at[c, a], 0, raw_sem.at[c, a], partner).wait_recv()
            own, other = raw_own[c, a], raw_other[c, a]
            cells = jnp.concatenate([jnp.where(lower, own, other), jnp.where(lower, other, own)], axis=0)
            freqs = table_left(y_tab[0], y_tab[1], cells)
            count = blocks * 2 * each
            for part in range(PARTS):
                start = (part * CHUNKS + c) * blocks * piece + a
                f_sent[pl.ds(start, count, stride=rows), :] = freqs[part * count : (part + 1) * count]
            return 0

        lax.fori_loop(0, rows, body, 0)

    for c in range(CHUNKS):
        transform(c)
        send_plane(f_sent, f_got, 1, f_sem, 0, c)
    for part in range(1, PARTS):
        for c in range(CHUNKS):
            send_plane(f_sent, f_got, 1, f_sem, part, c)

    def green_copy(u):
        return remote(green_sent.at[u], green_other.at[u], 2, green_sem.at[u], partner)

    distant_copy = remote(nyquist, distant, 3, green_sem.at[units], partner)
    green_copy(0).start()

    @pl.when(block + (1 - gy) == 0)
    def _():
        distant_copy.start()

    for u in range(1, units):
        green_copy(u).start()

    def forward(r0, r1, i0, i1):
        mixes = [(r0 + r1, i0 + i1), (r0 + i1, i0 - r1), (r0 - r1, i0 - i1), (r0 - i1, i0 + r1)]
        out = []
        for m, (real, imag) in enumerate(mixes):
            o = table_left(x_tab[0, m], x_tab[1, m], jnp.concatenate([real, imag], axis=0))
            out.append(jnp.concatenate([o[:quarter], o[quarter:]], axis=1))
        out = jnp.concatenate(out, axis=0)
        return [table_right(out, z_tab[0, h], z_tab[1, h]) for h in (gy, 1 - gy)]

    def unit_step(u, _):
        part, c = u // each, lax.rem(u, each)
        here = jnp.logical_and(packed, u == 0)

        @pl.when(c == 0)
        def _():
            for chunk in range(CHUNKS):
                wait_plane(f_got, 1, f_sem, part, chunk)

        def place(chunk, at, q):
            start = ((part * CHUNKS + chunk) * blocks + at) * piece + (2 * c + q) * rows
            return pl.ds(pl.multiple_of(start, 8), rows)

        for x in range(size_gx):
            for chunk in range(CHUNKS):
                for q in range(2):
                    pieces = [f_got[place(chunk, x * size_gz + g, q), :] for g in range(size_gz)]
                    at = q * half_x + (x * CHUNKS + chunk) * step_x
                    for b, moved in enumerate(block_swap(pieces, width)):
                        lines[at + b * rows : at + (b + 1) * rows] = moved

        field = lines[...]
        r0, r1 = field[:quarter], field[quarter:half_x]
        i0, i1 = field[half_x : half_x + quarter], field[half_x + quarter :]
        freqs = forward(r0, r1, jnp.where(here, 0.0, i0), jnp.where(here, 0.0, i1))
        green_copy(u).wait_recv()
        for side, gains in enumerate((green_own, green_other)):
            gain = gains[u].reshape(4 * quarter, share)
            spectrum[side] = jnp.concatenate([gain, gain], axis=1) * freqs[side]

        @pl.when(here)
        def _():
            distant_copy.wait_recv()
            i0 = lines[half_x : half_x + quarter]
            i1 = lines[half_x + quarter : 2 * half_x]
            zero = jnp.zeros_like(i0)
            for side, freqs in enumerate(forward(zero, zero, i0, i1)):
                gain = (nyquist, distant)[side][...].reshape(4 * quarter, share)
                spectrum[side] += jnp.concatenate([gain, gain], axis=1) * freqs

        inverse = sum(
            table_right(spectrum[side], z_back[0, h], z_back[1, h]) for side, h in ((0, gy), (1, 1 - gy))
        )
        near_r = near_i = far_r = far_i = 0.0
        for m in range(4):
            out = inverse[m * quarter : (m + 1) * quarter]
            both = jnp.concatenate([out[:, :LANES], out[:, LANES:]], axis=0)
            o = table_left(x_back[0, m], x_back[1, m], both)
            real, imag = o[:quarter], o[quarter:]
            near_r, near_i = near_r + real, near_i + imag
            turn_r, turn_i = [(real, imag), (-imag, real), (-real, -imag), (imag, -real)][m]
            far_r, far_i = far_r + turn_r, far_i + turn_i
        lines[...] = jnp.concatenate([near_r, far_r, near_i, far_i], axis=0)

        for x in range(size_gx):
            for chunk in range(CHUNKS):
                for q in range(2):
                    at = q * half_x + (x * CHUNKS + chunk) * step_x
                    pieces = [lines[at + b * rows : at + (b + 1) * rows] for b in range(group)]
                    for g, moved in enumerate(block_swap(pieces, width)):
                        b_sent[place(chunk, x * size_gz + g, q), :] = moved

        @pl.when(c == each - 1)
        def _():
            for chunk in range(CHUNKS):
                send_plane(b_sent, b_got, 4, b_sem, part, chunk)

        return 0

    lax.fori_loop(0, units, unit_step, 0)

    def part_copy(c, a):
        return remote(part_sent.at[c, a], part_other.at[c, a], 5, part_sem.at[c, a], partner)

    def invert(c):
        for part in range(PARTS):
            wait_plane(b_got, 4, b_sem, part, c)

        def body(a, _):
            count = blocks * 2 * each
            freqs = jnp.concatenate(
                [
                    b_got[pl.ds((part * CHUNKS + c) * blocks * piece + a, count, stride=rows), :]
                    for part in range(PARTS)
                ],
                axis=0,
            )
            cells = table_left(y_back[0], y_back[1], freqs)
            low, high = cells[:count_y], cells[count_y:]
            part_sent[c, a] = jnp.where(lower, high, low)
            part_own[c, a] = jnp.where(lower, low, high)
            part_copy(c, a).start()
            return 0

        lax.fori_loop(0, rows, body, 0)

    for c in range(CHUNKS):
        invert(c)

    for c in range(CHUNKS):
        def finish(a, _):
            part_copy(c, a).wait_recv()
            out_ref[c * rows + a] = part_own[c, a] + part_other[c, a]
            return 0

        lax.fori_loop(0, rows, finish, 0)

    remote(raw_own, raw_other, 0, raw_sem.at[0, 0], partner).wait_send()
    moved = f_sent.at[pl.ds(0, PARTS * CHUNKS * (blocks - 1) * piece), :]
    remote(moved, moved, 1, f_sem.at[0, 0], partner).wait_send()
    remote(green_sent, green_other, 2, green_sem.at[0], partner).wait_send()

    @pl.when(block + (1 - gy) == 0)
    def _():
        distant_copy.wait_send()

    remote(moved, moved, 4, b_sem.at[0, 0], partner).wait_send()
    remote(part_sent, part_other, 5, part_sem.at[0, 0], partner).wait_send()


def unpack_kernel(in_ref, out_ref):
    width = out_ref.shape[1]
    group = LANES // width
    for row in range(in_ref.shape[0]):
        block = in_ref[row].T
        for b in range(group):
            out_ref[row * group + b] = block[b * width : (b + 1) * width]


def f32(*shape):
    return jax.ShapeDtypeStruct(shape, jnp.float32)


def fast_device(source, green):
    size_gx = lax.axis_size("gx")
    size_gy = lax.axis_size("gy")
    size_gz = lax.axis_size("gz")
    brick_x, brick_y, brick_z = source.shape
    long_x, places, share = green.shape
    long_y = 2 * brick_y * size_gy
    long_z = 2 * brick_z * size_gz
    blocks = size_gx * size_gz
    units = places // (2 * size_gy)
    group = LANES // brick_z
    rows = brick_x // group // CHUNKS
    quarter = long_x // 4
    y_tab, y_back = y_tables(long_y, blocks, units, 1.0 / (long_x * long_z))
    x_tab, z_tab = x_table(long_x, group, rows), z_table(long_z, 2)
    lines = blocks * units * 2 * CHUNKS * rows
    vmem = lambda *shape: pltpu.VMEM(shape, jnp.float32)
    half = lambda *shape: pltpu.VMEM(shape, jnp.bfloat16)
    raw = (CHUNKS, rows, brick_y, LANES)
    slots = (units, 4, quarter, share)
    parts = pl.pallas_call(
        functools.partial(whole_kernel, size_gx, size_gz, units),
        out_shape=f32(CHUNKS * rows, brick_y, LANES),
        in_specs=[pl.BlockSpec(memory_space=pltpu.HBM)] * 6,
        out_specs=pl.BlockSpec(memory_space=pltpu.VMEM),
        scratch_shapes=[
            vmem(brick_x, brick_z, brick_y),
            vmem(long_x * places, share),
            half(*y_tab.shape[1:]),
            half(*y_back.shape[1:]),
            half(*x_tab.shape),
            half(*z_tab.shape),
            half(2, 4, 2 * quarter, 2 * quarter),
            half(2, 4, 2 * quarter, 2 * quarter),
            half(2, 2, long_z, 2 * share),
            half(2, 2, long_z, 2 * share),
            vmem(*raw),
            vmem(*raw),
            vmem(*slots),
            vmem(*slots),
            vmem(*slots),
            vmem(*slots[1:]),
            vmem(*slots[1:]),
            vmem(lines, LANES),
            vmem(lines, LANES),
            vmem(lines, LANES),
            vmem(lines, LANES),
            vmem(long_x, LANES),
            vmem(2, long_x, 2 * share),
            vmem(*raw),
            vmem(*raw),
            vmem(*raw),
            pltpu.SemaphoreType.DMA((CHUNKS + 5,)),
            pltpu.SemaphoreType.DMA((6,)),
            pltpu.SemaphoreType.DMA((CHUNKS, rows)),
            pltpu.SemaphoreType.DMA((units + 1,)),
            pltpu.SemaphoreType.DMA((PARTS, CHUNKS)),
            pltpu.SemaphoreType.DMA((PARTS, CHUNKS)),
            pltpu.SemaphoreType.DMA((CHUNKS, rows)),
        ],
        compiler_params=pltpu.CompilerParams(
            vmem_limit_bytes=VMEM_BYTES, collective_id=0, has_side_effects=True
        ),
    )(jnp.swapaxes(source, 1, 2), green.reshape(long_x * places, share), y_tab, y_back, x_tab, z_tab)
    result = pl.pallas_call(
        unpack_kernel,
        out_shape=f32(brick_x, brick_z, brick_y),
        compiler_params=pltpu.CompilerParams(vmem_limit_bytes=VMEM_BYTES),
    )(parts)
    return jnp.swapaxes(result, 1, 2)


def fits(sizes, source, green):
    brick_x, brick_y, brick_z = source.shape
    units = green.shape[1] // (2 * sizes["gy"])
    return (
        brick_z * sizes["gz"] == LANES
        and green.shape[2] == LANES
        and sizes["gx"] * brick_x == 2 * LANES
        and brick_y * sizes["gy"] == LANES
        and brick_x * brick_z == 8 * CHUNKS * LANES
        and units % PARTS == 0
        and sizes["gy"] == 2
    )


def phase_table(row_index, column_index, length):
    phase_index = row_index[:, None] * column_index[None, :] % length
    angles = phase_index.astype(jnp.float32) * (2.0 * math.pi / length)
    return (jnp.cos(angles), jnp.sin(angles))


def pair_frequency(position, length):
    unit_index = position // 2
    member = position % 2
    return jnp.where(
        unit_index == 0,
        member * (length // 2),
        jnp.where(member == 0, unit_index, length - unit_index),
    )


def product(form, left, table):
    return jnp.einsum(form, left, table, precision=lax.Precision.HIGHEST)


def mirror_plane(field, first_block):
    flipped = jnp.roll(jnp.flip(field, 1), 1, 1)
    count_y, count_x = field.shape
    swapped = flipped.reshape(count_y // 2, 2, count_x)[:, ::-1, :].reshape(count_y, count_x)
    local_row = lax.iota(jnp.int32, count_y)
    keep_unit = jnp.logical_and(first_block, local_row < 2)
    return jnp.where(keep_unit[:, None], flipped, swapped)


def per_device(source, green):
    size_gx = lax.axis_size("gx")
    size_gy = lax.axis_size("gy")
    size_gz = lax.axis_size("gz")
    brick_x, brick_y, brick_z = source.shape
    if fits({"gx": size_gx, "gy": size_gy, "gz": size_gz}, source, green):
        return fast_device(source, green)
    grid_x = brick_x * size_gx
    grid_y = brick_y * size_gy
    grid_z = brick_z * size_gz
    long_x = 2 * grid_x
    long_y = 2 * grid_y
    long_z = 2 * grid_z
    cell_z = lax.iota(jnp.int32, grid_z)
    parity_sign = (1 - 2 * (cell_z % 2)).astype(jnp.float32)
    z_lines = lax.all_to_all(source, "gz", split_axis=0, concat_axis=2, tiled=True)
    kept_freq = lax.iota(jnp.int32, long_z // 2)
    z_cos, z_sin = phase_table(cell_z, kept_freq, long_z)
    z_sin = jnp.where(kept_freq[None, :] == 0, -parity_sign[:, None], z_sin)
    z_real = product("abn,nk->abk", z_lines, z_cos)
    z_imag = -product("abn,nk->abk", z_lines, z_sin)
    y_real, y_imag = (
        lax.all_to_all(z_real, "gy", split_axis=2, concat_axis=1, tiled=True),
        lax.all_to_all(z_imag, "gy", split_axis=2, concat_axis=1, tiled=True),
    )
    y_cos, y_sin = phase_table(
        lax.iota(jnp.int32, grid_y), pair_frequency(lax.iota(jnp.int32, long_y), long_y), long_y
    )
    fy_real = product("ayc,yk->ack", y_real, y_cos) + product("ayc,yk->ack", y_imag, y_sin)
    fy_imag = product("ayc,yk->ack", y_imag, y_cos) - product("ayc,yk->ack", y_real, y_sin)
    x_real, x_imag = (
        lax.all_to_all(fy_real, ("gx", "gz"), split_axis=2, concat_axis=0, tiled=True),
        lax.all_to_all(fy_imag, ("gx", "gz"), split_axis=2, concat_axis=0, tiled=True),
    )
    x_rows = lax.iota(jnp.int32, grid_x)
    x_cos, x_sin = phase_table(x_rows, lax.iota(jnp.int32, long_x), long_x)
    full_real = product("xck,xj->ckj", x_real, x_cos) + product("xck,xj->ckj", x_imag, x_sin)
    full_imag = product("xck,xj->ckj", x_imag, x_cos) - product("xck,xj->ckj", x_real, x_sin)
    kept_green = jnp.transpose(green[:, :, 0::2], (2, 1, 0))
    nyquist_green = jnp.transpose(green[:, :, 1], (1, 0))
    prod_real = kept_green * full_real
    prod_imag = kept_green * full_imag
    first_block = lax.axis_index("gx") * size_gz + lax.axis_index("gz") == 0
    first_slab = lax.axis_index("gy") == 0
    base_real = full_real[0]
    base_imag = full_imag[0]
    mirror_real = mirror_plane(base_real, first_block)
    mirror_imag = mirror_plane(base_imag, first_block)
    zero_real = 0.5 * (base_real + mirror_real)
    zero_imag = 0.5 * (base_imag - mirror_imag)
    nyq_real = 0.5 * (base_imag + mirror_imag)
    nyq_imag = 0.5 * (mirror_real - base_real)
    zero_green = kept_green[0]
    packed_real = zero_green * zero_real - nyquist_green * nyq_imag
    packed_imag = zero_green * zero_imag + nyquist_green * nyq_real
    slot_mask = jnp.logical_and(lax.iota(jnp.int32, prod_real.shape[0]) == 0, first_slab)
    prod_real = jnp.where(slot_mask[:, None, None], packed_real[None], prod_real)
    prod_imag = jnp.where(slot_mask[:, None, None], packed_imag[None], prod_imag)
    inv_xcos, inv_xsin = phase_table(
        lax.iota(jnp.int32, long_x), lax.iota(jnp.int32, grid_x), long_x
    )
    back_real = (
        product("ckj,jx->ckx", prod_real, inv_xcos) - product("ckj,jx->ckx", prod_imag, inv_xsin)
    ) / long_x
    back_imag = (
        product("ckj,jx->ckx", prod_imag, inv_xcos) + product("ckj,jx->ckx", prod_real, inv_xsin)
    ) / long_x
    mid_real, mid_imag = (
        lax.all_to_all(back_real, ("gx", "gz"), split_axis=2, concat_axis=1, tiled=True),
        lax.all_to_all(back_imag, ("gx", "gz"), split_axis=2, concat_axis=1, tiled=True),
    )
    y_order = lax.iota(jnp.int32, long_y)
    inv_ycos, inv_ysin = phase_table(
        pair_frequency(y_order, long_y), lax.iota(jnp.int32, grid_y), long_y
    )
    half_real = (
        product("cja,jy->cay", mid_real, inv_ycos) - product("cja,jy->cay", mid_imag, inv_ysin)
    ) / long_y
    half_imag = (
        product("cja,jy->cay", mid_imag, inv_ycos) + product("cja,jy->cay", mid_real, inv_ysin)
    ) / long_y
    last_real, last_imag = (
        lax.all_to_all(half_real, "gy", split_axis=2, concat_axis=0, tiled=True),
        lax.all_to_all(half_imag, "gy", split_axis=2, concat_axis=0, tiled=True),
    )
    kept_freq = lax.iota(jnp.int32, long_z // 2)
    base_cos, base_sin = phase_table(kept_freq, cell_z, long_z)
    inv_zcos = jnp.where(kept_freq[:, None] == 0, 1.0, 2.0 * base_cos)
    inv_zsin = jnp.where(kept_freq[:, None] == 0, -parity_sign[None, :], 2.0 * base_sin)
    result = (
        product("jab,jn->abn", last_real, inv_zcos) - product("jab,jn->abn", last_imag, inv_zsin)
    ) / long_z
    return lax.all_to_all(result, "gz", split_axis=2, concat_axis=0, tiled=True)


def solution(mesh):
    step = jax.shard_map(
        per_device,
        mesh=mesh,
        in_specs=(P("gx", "gy", "gz"), P(None, ("gx", "gz"), "gy")),
        out_specs=P("gx", "gy", "gz"),
        check_vma=False,
    )
    return step
```

profile of v0, /device:TPU:0, one launch (start us, length us, event | category | flops | bytes accessed | tf_op | source)
XLA Modules:
  0.0 75.1 jit_solution(5626432881768705219)
XLA Ops:
  0.0 0.0 copy-start
  0.0 1.2 %copy-done = f32[64,64,32]{1,2,0:T(8,128)S(1)} copy-done((f32[64,64,32]{1,2,0:T(8,128)S(1)}, f32[64,64,32]{1,2,0:T(8,128)}, u32[]{:S(2)}) %copy-start) | copy-done | bytes 524312
  1.2 0.0 copy-start.1
  1.2 1.0 %copy-done.1 = bf16[2,4,128,256]{3,2,1,0:T(8,128)(2,1)S(1)} copy-done((bf16[2,4,128,256]{3,2,1,0:T(8,128)(2,1)S(1)}, bf16[2,4,128,256]{3,2,1,0:T(8,128)(2,1)}, u32[]{:S(2)}) %copy-start.1) | copy-done | bytes 524312
  2.3 0.0 copy-start.2
  2.3 0.9 %copy-done.2 = bf16[2,2,128,256]{3,2,1,0:T(8,128)(2,1)S(1)} copy-done((bf16[2,2,128,256]{3,2,1,0:T(8,128)(2,1)S(1)}, bf16[2,2,128,256]{3,2,1,0:T(8,128)(2,1)}, u32[]{:S(2)}) %copy-start.2) | copy-done | bytes 262168
  3.2 0.0 copy-start.3
  3.2 0.9 %copy-done.3 = bf16[2,2,128,128]{3,2,1,0:T(8,128)(2,1)S(1)} copy-done((bf16[2,2,128,128]{3,2,1,0:T(8,128)(2,1)S(1)}, bf16[2,2,128,128]{3,2,1,0:T(8,128)(2,1)}, u32[]{:S(2)}) %copy-start.3) | copy-done | bytes 131096
  4.1 0.0 copy-start.4
  4.1 0.9 %copy-done.4 = bf16[2,2,128,128]{3,2,1,0:T(8,128)(2,1)S(1)} copy-done((bf16[2,2,128,128]{3,2,1,0:T(8,128)(2,1)S(1)}, bf16[2,2,128,128]{3,2,1,0:T(8,128)(2,1)}, u32[]{:S(2)}) %copy-start.4) | copy-done | bytes 131096
  5.0 68.7 %shard_map.64.in_ref = f32[16,64,128]{2,1,0:T(8,128)S(1)} custom-call(f32[64,32,64]{2,1,0:T(8,128)S(1)} %bitcast.3, f32[8192,128]{1,0:T(8,128)} %bitcast.4, bf16[2,2,128,128]{3,2,1,0:T(8,128)(2,1)S(1)} %copy-done.4, bf16[2,2,128,128]{3,2,1,0:T(8,128)(2,1)S(1)} %copy-done.3, bf16[2,4,128,256]{3,2,1,0:T(8,128)(2,1)S(1)} %copy-done.1, ...), custom_call_target="tpu_custom_call" | custom-call | tf_op jit(solution)/shard_map/pallas_call | solution.py:430
  73.7 1.3 %shard_map.65 = f32[64,32,64]{2,1,0:T(8,128)} custom-call(f32[16,64,128]{2,1,0:T(8,128)S(1)} %shard_map.64.in_ref), custom_call_target="tpu_custom_call" | custom-call | tf_op jit(solution)/shard_map/pallas_call | solution.py:474
Async XLA Ops:
  0.0 1.2 %copy-start = (f32[64,64,32]{1,2,0:T(8,128)S(1)}, f32[64,64,32]{1,2,0:T(8,128)}, u32[]{:S(2)}) copy-start(f32[64,64,32]{1,2,0:T(8,128)} %param.6) | copy-start | bytes 1572868
  1.2 1.0 %copy-start.1 = (bf16[2,4,128,256]{3,2,1,0:T(8,128)(2,1)S(1)}, bf16[2,4,128,256]{3,2,1,0:T(8,128)(2,1)}, u32[]{:S(2)}) copy-start(bf16[2,4,128,256]{3,2,1,0:T(8,128)(2,1)} %constant.10.clone.x_hbm) | copy-start | bytes 1572868
  2.3 0.9 %copy-start.2 = (bf16[2,2,128,256]{3,2,1,0:T(8,128)(2,1)S(1)}, bf16[2,2,128,256]{3,2,1,0:T(8,128)(2,1)}, u32[]{:S(2)}) copy-start(bf16[2,2,128,256]{3,2,1,0:T(8,128)(2,1)} %constant.11.clone.z_hbm) | copy-start | bytes 786436
  3.2 0.9 %copy-start.3 = (bf16[2,2,128,128]{3,2,1,0:T(8,128)(2,1)S(1)}, bf16[2,2,128,128]{3,2,1,0:T(8,128)(2,1)}, u32[]{:S(2)}) copy-start(bf16[2,2,128,128]{3,2,1,0:T(8,128)(2,1)} %constant.9.clone.yback_hbm) | copy-start | bytes 393220
  4.1 0.9 %copy-start.4 = (bf16[2,2,128,128]{3,2,1,0:T(8,128)(2,1)S(1)}, bf16[2,2,128,128]{3,2,1,0:T(8,128)(2,1)}, u32[]{:S(2)}) copy-start(bf16[2,2,128,128]{3,2,1,0:T(8,128)(2,1)} %constant.8.clone.y_hbm) | copy-start | bytes 393220
where the time goes:
time: 76.1 us; the launch traced here: 75.1 us
  Pallas kernels  70 us (92%)
  local copies, waits for them, and re-layouts  5.02 us (7%)
    pallas_call x1, Pallas kernels, fast_device(): pl.pallas_call(functools.partial(whole_kernel, size_gx, size_gz, units),...  68.7 us
    unnamed x10, local copies, waits for them, and re-layouts  5.02 us

commit v1 on v0

--- a/solution.py
+++ b/solution.py
@@ -12,8 +12,8 @@
 
 LANES = 128
 PARTS = 2
-CHUNKS = 2
-VMEM_BYTES = 48 * 1024 * 1024
+CHUNKS = 4
+VMEM_BYTES = 63 * 1024 * 1024
 
 
 def np_halves(table):
@@ -80,15 +80,16 @@
 
 
 def x_table(length_x, group, rows):
-    freqs = np.arange(length_x // 4)
-    place = np.arange(length_x // 4)
-    block, rest = place // (group * rows), place % (group * rows)
-    cells = block * group * rows + rest % rows * group + rest // rows
+    freqs = np.arange(length_x // 4)[:, None]
+    place = np.arange(length_x // 2)[None, :]
+    a, q = place % rows, place // rows % 2
+    b, block = place // (2 * rows) % group, place // (2 * rows * group)
+    cells = (block * rows + a) * group + b
     out = []
     for member in range(4):
-        freq = 4 * freqs + member
-        angle = 2.0 * np.pi * (np.outer(freq, cells) % length_x) / length_x
-        out.append(np.concatenate([np.cos(angle), np.sin(angle)], 1))
+        angle = 2.0 * np.pi * ((4 * freqs + member) * cells % length_x) / length_x
+        c, s = np.cos(angle), np.sin(angle)
+        out.append(np.concatenate([np.where(q == 0, c, s), np.where(q == 0, -s, c)], 0))
     return np_halves(np.stack(out))
 
 
@@ -105,22 +106,28 @@
 
 
 def expand(source, out, back):
-    size = source.shape[2]
-    for part in range(2):
-        for m in range(source.shape[1]):
-            c = source[part, m, :, :size].astype(jnp.float32)
-            s = source[part, m, :, size:].astype(jnp.float32)
-            full = jnp.concatenate(
-                [jnp.concatenate([c, s], axis=1), jnp.concatenate([-s, c], axis=1)], axis=0
-            )
-            out[part, m] = full.astype(jnp.bfloat16)
-            back[part, m] = full.T.astype(jnp.bfloat16)
+    size = source.shape[1] // 2
+    for at in range(source.shape[0] // size):
+        c = source[at * size : (at + 1) * size, :size].astype(jnp.float32)
+        s = source[at * size : (at + 1) * size, size:].astype(jnp.float32)
+        full = jnp.concatenate(
+            [jnp.concatenate([c, s], axis=1), jnp.concatenate([-s, c], axis=1)], axis=0
+        )
+        out[at] = full.astype(jnp.bfloat16)
+        back[at] = full.T.astype(jnp.bfloat16)
+
+
+def transposed(source, back):
+    size = source.shape[1]
+    for at in range(source.shape[0] // size):
+        block = source[at * size : (at + 1) * size, :]
+        back[at] = block.astype(jnp.float32).T.astype(jnp.bfloat16)
 
 
 def whole_kernel(
     size_gx, size_gz, units,
-    source_hbm, green_hbm, y_hbm, yback_hbm, x_hbm, z_hbm, out_ref,
-    source, green, y_tab, y_back, x_half, z_half, x_tab, x_back, z_tab, z_back,
+    source_hbm, green_hbm, tables_hbm, out_ref,
+    source, green, y_both, x_tab, x_back, z_half, z_tab, z_back,
     raw_own, raw_other, green_own, green_sent, green_other, nyquist, distant,
     f_sent, f_got, b_sent, b_got, lines, spectrum, part_own, part_sent, part_other,
     local_sem, send_sem, raw_sem, green_sem, f_sem, b_sem, part_sem,
@@ -132,6 +139,7 @@
     width = LANES // group
     rows = raw_own.shape[1]
     count_y = raw_own.shape[2]
+    lines_y = 2 * count_y
     each = units // PARTS
     piece = 2 * each * rows
     share = green_own.shape[3]
@@ -180,13 +188,17 @@
         )
         for c in range(CHUNKS)
     ]
-    copies += [
-        pltpu.make_async_copy(green_hbm, green, local_sem.at[CHUNKS]),
-        pltpu.make_async_copy(x_hbm, x_half, local_sem.at[CHUNKS + 1]),
-        pltpu.make_async_copy(z_hbm, z_half, local_sem.at[CHUNKS + 2]),
-        pltpu.make_async_copy(y_hbm.at[gy], y_tab, local_sem.at[CHUNKS + 3]),
-        pltpu.make_async_copy(yback_hbm.at[gy], y_back, local_sem.at[CHUNKS + 4]),
-    ]
+    copies.append(pltpu.make_async_copy(green_hbm, green, local_sem.at[CHUNKS]))
+    start = 0
+    for n, (table, which) in enumerate(((x_tab, None), (z_half, None), (y_both, gy))):
+        size = table.shape[0]
+        at = start if which is None else start + which * size
+        copies.append(
+            pltpu.make_async_copy(
+                tables_hbm.at[pl.ds(at, size), :], table, local_sem.at[CHUNKS + 1 + n]
+            )
+        )
+        start += size
     for copy in copies:
         copy.start()
 
@@ -225,18 +237,17 @@
     for m in range(4):
         nyquist[m] = green[pl.ds(m * positions + 1, quarter, stride=4 * positions), :]
     copies[CHUNKS + 1].wait()
+    transposed(x_tab, x_back)
     copies[CHUNKS + 2].wait()
-    expand(x_half, x_tab, x_back)
     expand(z_half, z_tab, z_back)
     copies[CHUNKS + 3].wait()
-    copies[CHUNKS + 4].wait()
 
     def transform(c):
         def body(a, _):
             remote(raw_own.at[c, a], raw_other.at[c, a], 0, raw_sem.at[c, a], partner).wait_recv()
             own, other = raw_own[c, a], raw_other[c, a]
             cells = jnp.concatenate([jnp.where(lower, own, other), jnp.where(lower, other, own)], axis=0)
-            freqs = table_left(y_tab[0], y_tab[1], cells)
+            freqs = table_left(y_both[:lines_y, :lines_y], y_both[lines_y:, :lines_y], cells)
             count = blocks * 2 * each
             for part in range(PARTS):
                 start = (part * CHUNKS + c) * blocks * piece + a
@@ -265,14 +276,22 @@
     for u in range(1, units):
         green_copy(u).start()
 
-    def forward(r0, r1, i0, i1):
-        mixes = [(r0 + r1, i0 + i1), (r0 + i1, i0 - r1), (r0 - r1, i0 - i1), (r0 - i1, i0 + r1)]
+    def turned(value):
+        tiles = value.reshape(-1, 2 * rows, LANES)
+        real = lax.broadcasted_iota(jnp.int32, tiles.shape, 1) < rows
+        moved = pltpu.roll(tiles, rows, 1)
+        return jnp.where(real, moved, -moved).reshape(value.shape)
+
+    def forward(field):
+        near, far = field[:half_x], field[half_x:]
+        twist = turned(far)
         out = []
-        for m, (real, imag) in enumerate(mixes):
-            o = table_left(x_tab[0, m], x_tab[1, m], jnp.concatenate([real, imag], axis=0))
+        for m, cells in enumerate((near + far, near + twist, near - far, near - twist)):
+            high, low = (x_tab[(4 * part + m) * half_x : (4 * part + m + 1) * half_x, :] for part in range(2))
+            o = table_left(high, low, cells)
             out.append(jnp.concatenate([o[:quarter], o[quarter:]], axis=1))
         out = jnp.concatenate(out, axis=0)
-        return [table_right(out, z_tab[0, h], z_tab[1, h]) for h in (gy, 1 - gy)]
+        return [table_right(out, z_tab[h], z_tab[2 + h]) for h in (gy, 1 - gy)]
 
     def unit_step(u, _):
         part, c = u // each, lax.rem(u, each)
@@ -283,22 +302,25 @@
             for chunk in range(CHUNKS):
                 wait_plane(f_got, 1, f_sem, part, chunk)
 
-        def place(chunk, at, q):
-            start = ((part * CHUNKS + chunk) * blocks + at) * piece + (2 * c + q) * rows
-            return pl.ds(pl.multiple_of(start, 8), rows)
+        def place(chunk, at):
+            start = ((part * CHUNKS + chunk) * blocks + at) * piece + 2 * c * rows
+            return pl.ds(pl.multiple_of(start, 8), 2 * rows)
 
         for x in range(size_gx):
             for chunk in range(CHUNKS):
-                for q in range(2):
-                    pieces = [f_got[place(chunk, x * size_gz + g, q), :] for g in range(size_gz)]
-                    at = q * half_x + (x * CHUNKS + chunk) * step_x
-                    for b, moved in enumerate(block_swap(pieces, width)):
-                        lines[at + b * rows : at + (b + 1) * rows] = moved
-
-        field = lines[...]
-        r0, r1 = field[:quarter], field[quarter:half_x]
-        i0, i1 = field[half_x : half_x + quarter], field[half_x + quarter :]
-        freqs = forward(r0, r1, jnp.where(here, 0.0, i0), jnp.where(here, 0.0, i1))
+                pieces = [f_got[place(chunk, x * size_gz + g), :] for g in range(size_gz)]
+                at = (x * CHUNKS + chunk) * 2 * step_x
+                for b, moved in enumerate(block_swap(pieces, width)):
+                    lines[at + 2 * b * rows : at + 2 * (b + 1) * rows] = moved
+
+        def masked(keep_real):
+            field = lines[...]
+            tiles = field.reshape(-1, 2 * rows, LANES)
+            real = lax.broadcasted_iota(jnp.int32, tiles.shape, 1) < rows
+            keep = jnp.logical_or(real == keep_real, jnp.logical_not(here))
+            return jnp.where(keep, tiles, 0.0).reshape(field.shape)
+
+        freqs = forward(masked(True))
         green_copy(u).wait_recv()
         for side, gains in enumerate((green_own, green_other)):
             gain = gains[u].reshape(4 * quarter, share)
@@ -307,34 +329,28 @@
         @pl.when(here)
         def _():
             distant_copy.wait_recv()
-            i0 = lines[half_x : half_x + quarter]
-            i1 = lines[half_x + quarter : 2 * half_x]
-            zero = jnp.zeros_like(i0)
-            for side, freqs in enumerate(forward(zero, zero, i0, i1)):
+            for side, freqs in enumerate(forward(masked(False))):
                 gain = (nyquist, distant)[side][...].reshape(4 * quarter, share)
                 spectrum[side] += jnp.concatenate([gain, gain], axis=1) * freqs
 
         inverse = sum(
-            table_right(spectrum[side], z_back[0, h], z_back[1, h]) for side, h in ((0, gy), (1, 1 - gy))
+            table_right(spectrum[side], z_back[h], z_back[2 + h]) for side, h in ((0, gy), (1, 1 - gy))
         )
-        near_r = near_i = far_r = far_i = 0.0
+        cells = []
         for m in range(4):
             out = inverse[m * quarter : (m + 1) * quarter]
             both = jnp.concatenate([out[:, :LANES], out[:, LANES:]], axis=0)
-            o = table_left(x_back[0, m], x_back[1, m], both)
-            real, imag = o[:quarter], o[quarter:]
-            near_r, near_i = near_r + real, near_i + imag
-            turn_r, turn_i = [(real, imag), (-imag, real), (-real, -imag), (imag, -real)][m]
-            far_r, far_i = far_r + turn_r, far_i + turn_i
-        lines[...] = jnp.concatenate([near_r, far_r, near_i, far_i], axis=0)
+            cells.append(table_left(x_back[m], x_back[4 + m], both))
+        even, odd = cells[0] + cells[2], cells[1] + cells[3]
+        lines[:half_x] = even + odd
+        lines[half_x:] = (cells[0] - cells[2]) - turned(cells[1] - cells[3])
 
         for x in range(size_gx):
             for chunk in range(CHUNKS):
-                for q in range(2):
-                    at = q * half_x + (x * CHUNKS + chunk) * step_x
-                    pieces = [lines[at + b * rows : at + (b + 1) * rows] for b in range(group)]
-                    for g, moved in enumerate(block_swap(pieces, width)):
-                        b_sent[place(chunk, x * size_gz + g, q), :] = moved
+                at = (x * CHUNKS + chunk) * 2 * step_x
+                pieces = [lines[at + 2 * b * rows : at + 2 * (b + 1) * rows] for b in range(group)]
+                for g, moved in enumerate(block_swap(pieces, width)):
+                    b_sent[place(chunk, x * size_gz + g), :] = moved
 
         @pl.when(c == each - 1)
         def _():
@@ -361,7 +377,7 @@
                 ],
                 axis=0,
             )
-            cells = table_left(y_back[0], y_back[1], freqs)
+            cells = table_left(y_both[:lines_y, lines_y:], y_both[lines_y:, lines_y:], freqs)
             low, high = cells[:count_y], cells[count_y:]
             part_sent[c, a] = jnp.where(lower, high, low)
             part_own[c, a] = jnp.where(lower, low, high)
@@ -422,6 +438,9 @@
     quarter = long_x // 4
     y_tab, y_back = y_tables(long_y, blocks, units, 1.0 / (long_x * long_z))
     x_tab, z_tab = x_table(long_x, group, rows), z_table(long_z, 2)
+    flat = lambda table: table.reshape(-1, 2 * share)
+    y_both = np.concatenate([y_tab, y_back], axis=3)
+    tables = np.concatenate([flat(x_tab), flat(z_tab), flat(y_both)])
     lines = blocks * units * 2 * CHUNKS * rows
     vmem = lambda *shape: pltpu.VMEM(shape, jnp.float32)
     half = lambda *shape: pltpu.VMEM(shape, jnp.bfloat16)
@@ -430,19 +449,17 @@
     parts = pl.pallas_call(
         functools.partial(whole_kernel, size_gx, size_gz, units),
         out_shape=f32(CHUNKS * rows, brick_y, LANES),
-        in_specs=[pl.BlockSpec(memory_space=pltpu.HBM)] * 6,
+        in_specs=[pl.BlockSpec(memory_space=pltpu.HBM)] * 3,
         out_specs=pl.BlockSpec(memory_space=pltpu.VMEM),
         scratch_shapes=[
             vmem(brick_x, brick_z, brick_y),
             vmem(long_x * places, share),
-            half(*y_tab.shape[1:]),
-            half(*y_back.shape[1:]),
-            half(*x_tab.shape),
-            half(*z_tab.shape),
-            half(2, 4, 2 * quarter, 2 * quarter),
-            half(2, 4, 2 * quarter, 2 * quarter),
-            half(2, 2, long_z, 2 * share),
-            half(2, 2, long_z, 2 * share),
+            half(*flat(y_both[0]).shape),
+            half(*flat(x_tab).shape),
+            half(8, 2 * quarter, 2 * quarter),
+            half(*flat(z_tab).shape),
+            half(4, long_z, 2 * share),
+            half(4, long_z, 2 * share),
             vmem(*raw),
             vmem(*raw),
             vmem(*slots),
@@ -459,7 +476,7 @@
             vmem(*raw),
             vmem(*raw),
             vmem(*raw),
-            pltpu.SemaphoreType.DMA((CHUNKS + 5,)),
+            pltpu.SemaphoreType.DMA((CHUNKS + 4,)),
             pltpu.SemaphoreType.DMA((6,)),
             pltpu.SemaphoreType.DMA((CHUNKS, rows)),
             pltpu.SemaphoreType.DMA((units + 1,)),
@@ -470,7 +487,7 @@
         compiler_params=pltpu.CompilerParams(
             vmem_limit_bytes=VMEM_BYTES, collective_id=0, has_side_effects=True
         ),
-    )(jnp.swapaxes(source, 1, 2), green.reshape(long_x * places, share), y_tab, y_back, x_tab, z_tab)
+    )(jnp.swapaxes(source, 1, 2), green.reshape(long_x * places, share), tables)
     result = pl.pallas_call(
         unpack_kernel,
         out_shape=f32(brick_x, brick_z, brick_y),
@@ -487,7 +504,7 @@
         and green.shape[2] == LANES
         and sizes["gx"] * brick_x == 2 * LANES
         and brick_y * sizes["gy"] == LANES
-        and brick_x * brick_z == 8 * CHUNKS * LANES
+        and brick_x * brick_z == 4 * CHUNKS * LANES
         and units % PARTS == 0
         and sizes["gy"] == 2
     )

time: 76.1 us -> 70 us (0.920); the launches traced: 75.1 us -> 69.8 us
  local copies, waits for them, and re-layouts: 5.02 us -> 0 us
    unnamed x10 -> x0, local copies, waits for them, and re-layouts: 5.02 us -> none
    pallas_call x1, Pallas kernels: 68.7 us -> 67.5 us  [fast_device(): pl.pallas_call(functools.partial(whole_kernel, size_gx, size_gz, units),...]
    pallas_call x1, Pallas kernels: 1.31 us -> 2.35 us  [fast_device(): pl.pallas_call(unpack_kernel, out_shape=f32(brick_x, brick_z, brick_y), c...]
where the time goes in v1:
time: 70 us; the launch traced here: 69.8 us
  Pallas kernels  69.8 us (100%)
    pallas_call x1, Pallas kernels, fast_device(): pl.pallas_call(functools.partial(whole_kernel, size_gx, size_gz, units),...  67.5 us
    pallas_call x1, Pallas kernels, fast_device(): pl.pallas_call(unpack_kernel, out_shape=f32(brick_x, brick_z, brick_y), c...  2.35 us

profile of v1, /device:TPU:0, one launch (start us, length us, event | category | flops | bytes accessed | tf_op | source)
XLA Modules:
  0.0 69.8 jit_solution(5506704794499142470)
XLA Ops:
  0.0 67.5 %shard_map.37.in_ref = f32[16,64,128]{2,1,0:T(8,128)} custom-call(f32[64,32,64]{2,1,0:T(8,128)} %bitcast.4, f32[8192,128]{1,0:T(8,128)} %bitcast.3, bf16[3072,256]{1,0:T(8,128)(2,1)} %constant.2.clone.tables_hbm), custom_call_target="tpu_custom_call" | custom-call | tf_op jit(solution)/shard_map/pallas_call | solution.py:449
  67.5 2.4 %shard_map.38 = f32[64,32,64]{2,1,0:T(8,128)} custom-call(f32[16,64,128]{2,1,0:T(8,128)} %shard_map.37.in_ref), custom_call_target="tpu_custom_call" | custom-call | tf_op jit(solution)/shard_map/pallas_call | solution.py:491

commit v2 on v1

--- a/solution.py
+++ b/solution.py
@@ -13,7 +13,7 @@
 LANES = 128
 PARTS = 2
 CHUNKS = 4
-VMEM_BYTES = 63 * 1024 * 1024
+VMEM_BYTES = 61 * 1024 * 1024
 
 
 def np_halves(table):
@@ -71,6 +71,7 @@
     back = both * weight[:, None]
 
     def ordered(table):
+        table = table.reshape(blocks, 2, units, 2, -1)[:, :, ::-1]
         table = table.reshape(blocks, 2, PARTS, units // PARTS, 2, -1)
         return table.transpose(1, 2, 0, 3, 4, 5).reshape(2, length_y // 2, -1)
 
@@ -217,10 +218,8 @@
         for a in range(rows):
             at = (c * rows + a) * group
             raw_own[c, a] = jnp.concatenate([source[at + b] for b in range(group)], axis=0).T
-
-    pl.semaphore_wait(barrier, blocks)
-
-    for c in range(CHUNKS):
+        if c == 0:
+            pl.semaphore_wait(barrier, blocks)
         for a in range(rows):
             remote(raw_own.at[c, a], raw_other.at[c, a], 0, raw_sem.at[c, a], partner).start()
 
@@ -229,13 +228,24 @@
     def extract(step, _):
         u, m = step // 4, lax.rem(step, 4)
         for half, out in ((gy, green_own), (1 - gy, green_sent)):
-            at = m * positions + 2 * (half * units + u)
+            at = m * positions + 2 * (half * units + units - 1 - u)
             out[u, m] = green[pl.ds(at, quarter, stride=4 * positions), :]
         return 0
 
     lax.fori_loop(0, 4 * units, extract, 0)
     for m in range(4):
         nyquist[m] = green[pl.ds(m * positions + 1, quarter, stride=4 * positions), :]
+    def green_copy(u):
+        return remote(green_sent.at[u], green_other.at[u], 2, green_sem.at[u], partner)
+
+    distant_copy = remote(nyquist, distant, 3, green_sem.at[units], partner)
+    for u in range(units):
+        green_copy(u).start()
+
+    @pl.when(block + (1 - gy) == 0)
+    def _():
+        distant_copy.start()
+
     copies[CHUNKS + 1].wait()
     transposed(x_tab, x_back)
     copies[CHUNKS + 2].wait()
@@ -263,19 +273,6 @@
         for c in range(CHUNKS):
             send_plane(f_sent, f_got, 1, f_sem, part, c)
 
-    def green_copy(u):
-        return remote(green_sent.at[u], green_other.at[u], 2, green_sem.at[u], partner)
-
-    distant_copy = remote(nyquist, distant, 3, green_sem.at[units], partner)
-    green_copy(0).start()
-
-    @pl.when(block + (1 - gy) == 0)
-    def _():
-        distant_copy.start()
-
-    for u in range(1, units):
-        green_copy(u).start()
-
     def turned(value):
         tiles = value.reshape(-1, 2 * rows, LANES)
         real = lax.broadcasted_iota(jnp.int32, tiles.shape, 1) < rows
@@ -295,7 +292,7 @@
 
     def unit_step(u, _):
         part, c = u // each, lax.rem(u, each)
-        here = jnp.logical_and(packed, u == 0)
+        here = jnp.logical_and(packed, u == units - 1)
 
         @pl.when(c == 0)
         def _():
@@ -328,8 +325,9 @@
 
         @pl.when(here)
         def _():
+            more = forward(masked(False))
             distant_copy.wait_recv()
-            for side, freqs in enumerate(forward(masked(False))):
+            for side, freqs in enumerate(more):
                 gain = (nyquist, distant)[side][...].reshape(4 * quarter, share)
                 spectrum[side] += jnp.concatenate([gain, gain], axis=1) * freqs
 
@@ -392,10 +390,13 @@
     for c in range(CHUNKS):
         def finish(a, _):
             part_copy(c, a).wait_recv()
-            out_ref[c * rows + a] = part_own[c, a] + part_other[c, a]
+            cells = (part_own[c, a] + part_other[c, a]).T
+            for b in range(group):
+                out_ref[(c * rows + a) * group + b] = cells[b * width : (b + 1) * width]
             return 0
 
         lax.fori_loop(0, rows, finish, 0)
+
 
     remote(raw_own, raw_other, 0, raw_sem.at[0, 0], partner).wait_send()
     moved = f_sent.at[pl.ds(0, PARTS * CHUNKS * (blocks - 1) * piece), :]
@@ -408,15 +409,6 @@
 
     remote(moved, moved, 4, b_sem.at[0, 0], partner).wait_send()
     remote(part_sent, part_other, 5, part_sem.at[0, 0], partner).wait_send()
-
-
-def unpack_kernel(in_ref, out_ref):
-    width = out_ref.shape[1]
-    group = LANES // width
-    for row in range(in_ref.shape[0]):
-        block = in_ref[row].T
-        for b in range(group):
-            out_ref[row * group + b] = block[b * width : (b + 1) * width]
 
 
 def f32(*shape):
@@ -446,9 +438,9 @@
     half = lambda *shape: pltpu.VMEM(shape, jnp.bfloat16)
     raw = (CHUNKS, rows, brick_y, LANES)
     slots = (units, 4, quarter, share)
-    parts = pl.pallas_call(
+    result = pl.pallas_call(
         functools.partial(whole_kernel, size_gx, size_gz, units),
-        out_shape=f32(CHUNKS * rows, brick_y, LANES),
+        out_shape=pltpu.VMEM((brick_x, brick_z, brick_y), jnp.float32),
         in_specs=[pl.BlockSpec(memory_space=pltpu.HBM)] * 3,
         out_specs=pl.BlockSpec(memory_space=pltpu.VMEM),
         scratch_shapes=[
@@ -488,11 +480,6 @@
             vmem_limit_bytes=VMEM_BYTES, collective_id=0, has_side_effects=True
         ),
     )(jnp.swapaxes(source, 1, 2), green.reshape(long_x * places, share), tables)
-    result = pl.pallas_call(
-        unpack_kernel,
-        out_shape=f32(brick_x, brick_z, brick_y),
-        compiler_params=pltpu.CompilerParams(vmem_limit_bytes=VMEM_BYTES),
-    )(parts)
     return jnp.swapaxes(result, 1, 2)
 
 

time: 70 us -> 66.8 us (0.954)
  Pallas kernels: 69.8 us -> 65.1 us
  local copies, waits for them, and re-layouts: 0 us -> 0.97 us
    pallas_call x1, Pallas kernels: 67.5 us -> 65.1 us  [fast_device(): pl.pallas_call(functools.partial(whole_kernel, size_gx, size_gz, units),...]
    pallas_call x1 -> x0, Pallas kernels: 2.35 us -> none  [fast_device(): pl.pallas_call(unpack_kernel, out_shape=f32(brick_x, brick_z, brick_y), c...]
    unnamed x0 -> x1, local copies, waits for them, and re-layouts: none -> 0.97 us
where the time goes in v2:
time: 66.8 us; the launch traced here: 66.1 us
  Pallas kernels  65.1 us (97%)
  local copies, waits for them, and re-layouts  0.97 us (1%)
    pallas_call x1, Pallas kernels, fast_device(): pl.pallas_call(functools.partial(whole_kernel, size_gx, size_gz, units),...  65.1 us

profile of v2, /device:TPU:0, one launch (start us, length us, event | category | flops | bytes accessed | tf_op | source)
XLA Modules:
  0.0 66.1 jit_solution(4034992550316797531)
XLA Ops:
  0.0 65.1 %shard_map.37 = f32[64,32,64]{2,1,0:T(8,128)S(1)} custom-call(f32[64,32,64]{2,1,0:T(8,128)} %bitcast.5, f32[8192,128]{1,0:T(8,128)} %bitcast.4, bf16[3072,256]{1,0:T(8,128)(2,1)} %constant.2.clone.tables_hbm), custom_call_target="tpu_custom_call" | custom-call | tf_op jit(solution)/shard_map/pallas_call | solution.py:441
  65.1 1.0 %copy.5 = f32[64,64,32]{1,2,0:T(8,128)} copy(f32[64,64,32]{1,2,0:T(8,128)S(1)} %bitcast.3) | data formatting | bytes 1048576

commit v3 on v2

--- a/solution.py
+++ b/solution.py
@@ -12,7 +12,8 @@
 
 LANES = 128
 PARTS = 2
-CHUNKS = 4
+CHUNKS = 8
+SENT = (3,5,6,7,8,8,8,8,8,8)
 VMEM_BYTES = 61 * 1024 * 1024
 
 
@@ -83,9 +84,9 @@
 def x_table(length_x, group, rows):
     freqs = np.arange(length_x // 4)[:, None]
     place = np.arange(length_x // 2)[None, :]
-    a, q = place % rows, place // rows % 2
-    b, block = place // (2 * rows) % group, place // (2 * rows * group)
-    cells = (block * rows + a) * group + b
+    a, q, h = place % rows, place // rows % 2, place // (2 * rows) % 2
+    b, block = place // (4 * rows) % group, place // (4 * rows * group)
+    cells = ((2 * block + h) * rows + a) * group + b
     out = []
     for member in range(4):
         angle = 2.0 * np.pi * ((4 * freqs + member) * cells % length_x) / length_x
@@ -130,7 +131,7 @@
     source_hbm, green_hbm, tables_hbm, out_ref,
     source, green, y_both, x_tab, x_back, z_half, z_tab, z_back,
     raw_own, raw_other, green_own, green_sent, green_other, nyquist, distant,
-    f_sent, f_got, b_sent, b_got, lines, spectrum, part_own, part_sent, part_other,
+    f_sent, f_got, b_sent, b_got, lines, extra, spectrum, part_own, part_sent, part_other,
     local_sem, send_sem, raw_sem, green_sem, f_sem, b_sem, part_sem,
 ):
     gx, gy, gz = lax.axis_index("gx"), lax.axis_index("gy"), lax.axis_index("gz")
@@ -161,27 +162,24 @@
         target = lax.rem(block + step, blocks)
         return target, {"gx": target // size_gz, "gz": lax.rem(target, size_gz)}
 
-    def span(part, chunk, at):
-        start = ((part * CHUNKS + chunk) * blocks + at) * piece
-        return pl.ds(pl.multiple_of(start, 8), piece)
-
-    def send_plane(sent_ref, got_ref, which, sems, part, chunk):
+    def send_plane(sent_ref, got_ref, which, sems, part, chunk, count):
+        at = pl.ds(part * CHUNKS + chunk, count)
+
         def body(step, _):
             target, device = plane_device(step)
             remote(
-                sent_ref.at[span(part, chunk, target), :],
-                got_ref.at[span(part, chunk, block), :],
-                which, sems.at[part, chunk], device,
+                sent_ref.at[at, target], got_ref.at[at, block], which, sems.at[part, chunk], device
             ).start()
             return 0
 
         lax.fori_loop(1, blocks, body, 0)
-        got_ref[span(part, chunk, block), :] = sent_ref[span(part, chunk, block), :]
-
-    def wait_plane(got_ref, which, sems, part, chunk):
-        everything = got_ref.at[pl.ds(0, (blocks - 1) * piece), :]
+        got_ref[at, block] = sent_ref[at, block]
+
+    def wait_plane(got_ref, which, sems, part, chunk, count):
+        everything = got_ref.at[pl.ds(0, count), pl.ds(0, blocks - 1)]
         remote(everything, everything, which, sems.at[part, chunk], partner).wait_recv()
 
+    flat = lambda ref: ref.reshape(PARTS * CHUNKS * blocks * piece, LANES)
     step_x = rows * group
     copies = [
         pltpu.make_async_copy(
@@ -235,16 +233,28 @@
     lax.fori_loop(0, 4 * units, extract, 0)
     for m in range(4):
         nyquist[m] = green[pl.ds(m * positions + 1, quarter, stride=4 * positions), :]
-    def green_copy(u):
-        return remote(green_sent.at[u], green_other.at[u], 2, green_sem.at[u], partner)
-
-    distant_copy = remote(nyquist, distant, 3, green_sem.at[units], partner)
-    for u in range(units):
+    def green_copy(u, sent=2):
+        return remote(green_sent.at[u], green_other.at[u], sent, green_sem.at[u], partner)
+
+    last = units - 1
+    some = pl.ds(0, quarter // 2 + 8)
+    plane_copy = remote(
+        green_sent.at[last, :, some], green_other.at[last, :, some], 6, green_sem.at[last], partner
+    )
+    distant_copy = remote(nyquist.at[:, some], distant.at[:, some], 3, green_sem.at[units], partner)
+    giver = block + (1 - gy) == 0
+
+    for u in range(last):
         green_copy(u).start()
 
-    @pl.when(block + (1 - gy) == 0)
+    @pl.when(giver)
     def _():
         distant_copy.start()
+        plane_copy.start()
+
+    @pl.when(jnp.logical_not(giver))
+    def _():
+        green_copy(last, 6).start()
 
     copies[CHUNKS + 1].wait()
     transposed(x_tab, x_back)
@@ -261,23 +271,28 @@
             count = blocks * 2 * each
             for part in range(PARTS):
                 start = (part * CHUNKS + c) * blocks * piece + a
-                f_sent[pl.ds(start, count, stride=rows), :] = freqs[part * count : (part + 1) * count]
+                flat(f_sent)[pl.ds(start, count, stride=rows), :] = freqs[part * count : (part + 1) * count]
             return 0
 
         lax.fori_loop(0, rows, body, 0)
 
     for c in range(CHUNKS):
         transform(c)
-        send_plane(f_sent, f_got, 1, f_sem, 0, c)
+        send_plane(f_sent, f_got, 1, f_sem, 0, c, 1)
     for part in range(1, PARTS):
-        for c in range(CHUNKS):
-            send_plane(f_sent, f_got, 1, f_sem, part, c)
+        send_plane(f_sent, f_got, 1, f_sem, part, 0, CHUNKS)
+
+    def tiled(value):
+        tiles = value.reshape(-1, 8, LANES)
+        return tiles, lax.broadcasted_iota(jnp.int32, tiles.shape, 1) // rows % 2 == 0
 
     def turned(value):
-        tiles = value.reshape(-1, 2 * rows, LANES)
-        real = lax.broadcasted_iota(jnp.int32, tiles.shape, 1) < rows
-        moved = pltpu.roll(tiles, rows, 1)
-        return jnp.where(real, moved, -moved).reshape(value.shape)
+        tiles, real = tiled(value)
+        return jnp.where(real, pltpu.roll(tiles, 8 - rows, 1), -pltpu.roll(tiles, rows, 1)).reshape(value.shape)
+
+    def chosen(where_real, where_imag):
+        left, real = tiled(where_real)
+        return jnp.where(real, left, tiled(where_imag)[0]).reshape(where_real.shape)
 
     def forward(field):
         near, far = field[:half_x], field[half_x:]
@@ -290,47 +305,11 @@
         out = jnp.concatenate(out, axis=0)
         return [table_right(out, z_tab[h], z_tab[2 + h]) for h in (gy, 1 - gy)]
 
-    def unit_step(u, _):
-        part, c = u // each, lax.rem(u, each)
-        here = jnp.logical_and(packed, u == units - 1)
-
-        @pl.when(c == 0)
-        def _():
-            for chunk in range(CHUNKS):
-                wait_plane(f_got, 1, f_sem, part, chunk)
-
-        def place(chunk, at):
-            start = ((part * CHUNKS + chunk) * blocks + at) * piece + 2 * c * rows
-            return pl.ds(pl.multiple_of(start, 8), 2 * rows)
-
-        for x in range(size_gx):
-            for chunk in range(CHUNKS):
-                pieces = [f_got[place(chunk, x * size_gz + g), :] for g in range(size_gz)]
-                at = (x * CHUNKS + chunk) * 2 * step_x
-                for b, moved in enumerate(block_swap(pieces, width)):
-                    lines[at + 2 * b * rows : at + 2 * (b + 1) * rows] = moved
-
-        def masked(keep_real):
-            field = lines[...]
-            tiles = field.reshape(-1, 2 * rows, LANES)
-            real = lax.broadcasted_iota(jnp.int32, tiles.shape, 1) < rows
-            keep = jnp.logical_or(real == keep_real, jnp.logical_not(here))
-            return jnp.where(keep, tiles, 0.0).reshape(field.shape)
-
-        freqs = forward(masked(True))
-        green_copy(u).wait_recv()
-        for side, gains in enumerate((green_own, green_other)):
-            gain = gains[u].reshape(4 * quarter, share)
+    def solve(field, gains_of):
+        freqs = forward(field)
+        for side, gain in enumerate(gains_of()):
+            gain = gain.reshape(4 * quarter, share)
             spectrum[side] = jnp.concatenate([gain, gain], axis=1) * freqs[side]
-
-        @pl.when(here)
-        def _():
-            more = forward(masked(False))
-            distant_copy.wait_recv()
-            for side, freqs in enumerate(more):
-                gain = (nyquist, distant)[side][...].reshape(4 * quarter, share)
-                spectrum[side] += jnp.concatenate([gain, gain], axis=1) * freqs
-
         inverse = sum(
             table_right(spectrum[side], z_back[h], z_back[2 + h]) for side, h in ((0, gy), (1, 1 - gy))
         )
@@ -340,37 +319,112 @@
             both = jnp.concatenate([out[:, :LANES], out[:, LANES:]], axis=0)
             cells.append(table_left(x_back[m], x_back[4 + m], both))
         even, odd = cells[0] + cells[2], cells[1] + cells[3]
-        lines[:half_x] = even + odd
-        lines[half_x:] = (cells[0] - cells[2]) - turned(cells[1] - cells[3])
-
-        for x in range(size_gx):
-            for chunk in range(CHUNKS):
-                at = (x * CHUNKS + chunk) * 2 * step_x
-                pieces = [lines[at + 2 * b * rows : at + 2 * (b + 1) * rows] for b in range(group)]
-                for g, moved in enumerate(block_swap(pieces, width)):
-                    b_sent[place(chunk, x * size_gz + g), :] = moved
-
-        @pl.when(c == each - 1)
+        far = (cells[0] - cells[2]) - turned(cells[1] - cells[3])
+        return jnp.concatenate([even + odd, far], axis=0)
+
+    def folded(gain):
+        m = lax.broadcasted_iota(jnp.int32, gain.shape, 0)
+        freq = 4 * lax.broadcasted_iota(jnp.int32, gain.shape, 1) + m
+        edge = jnp.logical_or(freq == 0, freq == 2 * quarter)
+        return jnp.where(edge, gain, jnp.where(freq < 2 * quarter, 2.0 * gain, 0.0))
+
+    def unit_step(part, c):
+        u = part * each + c
+        here = jnp.logical_and(packed, u == last)
+
+        def gains():
+            green_copy(u).wait_recv()
+            return green_own[u], green_other[u]
+
+        def plane_gains():
+            plane_copy.wait_recv()
+            return green_own[last], folded(green_other[last])
+
+        def distant_gains():
+            distant_copy.wait_recv()
+            return nyquist[...], folded(distant[...])
+
+        @pl.when(jnp.logical_not(here))
+        def _():
+            lines[c] = solve(lines[c], gains)
+
+        @pl.when(here)
+        def _():
+            field = lines[last % each]
+            zero = jnp.zeros_like(field)
+            extra[...] = solve(chosen(zero, field), distant_gains)
+            lines[last % each] = chosen(solve(chosen(lines[last % each], zero), plane_gains), extra[...])
+
+    def part_step(part, _):
+        @pl.when(part == 0)
         def _():
             for chunk in range(CHUNKS):
-                send_plane(b_sent, b_got, 4, b_sem, part, chunk)
+                wait_plane(f_got, 1, f_sem, 0, chunk, 1)
+
+        @pl.when(part > 0)
+        def _():
+            wait_plane(f_got, 1, f_sem, part, 0, CHUNKS)
+
+        first = lax.broadcasted_iota(jnp.int32, (8, LANES), 0) < 4
+        for x in range(size_gx):
+            for pair in range(CHUNKS // 2):
+                moved = []
+                for h in range(2):
+                    at = part * CHUNKS + 2 * pair + h
+                    moved.append(block_swap([f_got[at, x * size_gz + g] for g in range(size_gz)], width))
+                for b, (left, right) in enumerate(zip(*moved)):
+                    at = ((x * CHUNKS // 2 + pair) * group + b) * 8
+                    lines[0, at : at + 8] = jnp.where(first, left, pltpu.roll(right, 4, 0))
+                    lines[1, at : at + 8] = jnp.where(first, pltpu.roll(left, 4, 0), right)
+
+        def body(c, _):
+            unit_step(part, c)
+            return 0
+
+        lax.fori_loop(0, each, body, 0)
+
+        for x in range(size_gx):
+            for pair in range(CHUNKS // 2):
+                sides = ([], [])
+                for b in range(group):
+                    at = ((x * CHUNKS // 2 + pair) * group + b) * 8
+                    left, right = lines[0, at : at + 8], lines[1, at : at + 8]
+                    sides[0].append(jnp.where(first, left, pltpu.roll(right, 4, 0)))
+                    sides[1].append(jnp.where(first, pltpu.roll(left, 4, 0), right))
+                for h in range(2):
+                    at = part * CHUNKS + 2 * pair + h
+                    for g, moved in enumerate(block_swap(sides[h], width)):
+                        b_sent[at, x * size_gz + g] = moved
+
+        @pl.when(part < PARTS - 1)
+        def _():
+            send_plane(b_sent, b_got, 4, b_sem, part, 0, CHUNKS)
+
+        @pl.when(part == PARTS - 1)
+        def _():
+            for chunk in range(SENT[0]):
+                send_plane(b_sent, b_got, 4, b_sem, part, chunk, 1)
 
         return 0
 
-    lax.fori_loop(0, units, unit_step, 0)
+    lax.fori_loop(0, PARTS, part_step, 0)
+
+    def send_more(step):
+        for chunk in range(SENT[step], SENT[step + 1]):
+            send_plane(b_sent, b_got, 4, b_sem, PARTS - 1, chunk, 1)
 
     def part_copy(c, a):
         return remote(part_sent.at[c, a], part_other.at[c, a], 5, part_sem.at[c, a], partner)
 
     def invert(c):
-        for part in range(PARTS):
-            wait_plane(b_got, 4, b_sem, part, c)
+        wait_plane(b_got, 4, b_sem, PARTS - 1, c, 1)
+        send_more(c + 1)
 
         def body(a, _):
             count = blocks * 2 * each
             freqs = jnp.concatenate(
                 [
-                    b_got[pl.ds((part * CHUNKS + c) * blocks * piece + a, count, stride=rows), :]
+                    flat(b_got)[pl.ds((part * CHUNKS + c) * blocks * piece + a, count, stride=rows), :]
                     for part in range(PARTS)
                 ],
                 axis=0,
@@ -384,6 +438,9 @@
 
         lax.fori_loop(0, rows, body, 0)
 
+    for part in range(PARTS - 1):
+        wait_plane(b_got, 4, b_sem, part, 0, CHUNKS)
+    send_more(0)
     for c in range(CHUNKS):
         invert(c)
 
@@ -399,15 +456,21 @@
 
 
     remote(raw_own, raw_other, 0, raw_sem.at[0, 0], partner).wait_send()
-    moved = f_sent.at[pl.ds(0, PARTS * CHUNKS * (blocks - 1) * piece), :]
+    moved = f_sent.at[:, pl.ds(0, blocks - 1)]
     remote(moved, moved, 1, f_sem.at[0, 0], partner).wait_send()
-    remote(green_sent, green_other, 2, green_sem.at[0], partner).wait_send()
-
-    @pl.when(block + (1 - gy) == 0)
+    remote(moved, moved, 4, b_sem.at[0, 0], partner).wait_send()
+    most = green_sent.at[pl.ds(0, last)]
+    remote(most, most, 2, green_sem.at[0], partner).wait_send()
+
+    @pl.when(giver)
     def _():
         distant_copy.wait_send()
-
-    remote(moved, moved, 4, b_sem.at[0, 0], partner).wait_send()
+        plane_copy.wait_send()
+
+    @pl.when(jnp.logical_not(giver))
+    def _():
+        green_copy(last, 6).wait_send()
+
     remote(part_sent, part_other, 5, part_sem.at[0, 0], partner).wait_send()
 
 
@@ -433,7 +496,8 @@
     flat = lambda table: table.reshape(-1, 2 * share)
     y_both = np.concatenate([y_tab, y_back], axis=3)
     tables = np.concatenate([flat(x_tab), flat(z_tab), flat(y_both)])
-    lines = blocks * units * 2 * CHUNKS * rows
+    each = units // PARTS
+    plane = (PARTS * CHUNKS, blocks, 2 * each * rows, LANES)
     vmem = lambda *shape: pltpu.VMEM(shape, jnp.float32)
     half = lambda *shape: pltpu.VMEM(shape, jnp.bfloat16)
     raw = (CHUNKS, rows, brick_y, LANES)
@@ -459,17 +523,18 @@
             vmem(*slots),
             vmem(*slots[1:]),
             vmem(*slots[1:]),
-            vmem(lines, LANES),
-            vmem(lines, LANES),
-            vmem(lines, LANES),
-            vmem(lines, LANES),
+            vmem(*plane),
+            vmem(*plane),
+            vmem(*plane),
+            vmem(*plane),
+            vmem(each, long_x, LANES),
             vmem(long_x, LANES),
             vmem(2, long_x, 2 * share),
             vmem(*raw),
             vmem(*raw),
             vmem(*raw),
             pltpu.SemaphoreType.DMA((CHUNKS + 4,)),
-            pltpu.SemaphoreType.DMA((6,)),
+            pltpu.SemaphoreType.DMA((7,)),
             pltpu.SemaphoreType.DMA((CHUNKS, rows)),
             pltpu.SemaphoreType.DMA((units + 1,)),
             pltpu.SemaphoreType.DMA((PARTS, CHUNKS)),
@@ -491,8 +556,8 @@
         and green.shape[2] == LANES
         and sizes["gx"] * brick_x == 2 * LANES
         and brick_y * sizes["gy"] == LANES
-        and brick_x * brick_z == 4 * CHUNKS * LANES
-        and units % PARTS == 0
+        and brick_x * brick_z == 2 * CHUNKS * LANES
+        and units == 2 * PARTS
         and sizes["gy"] == 2
     )
 

time: 66.8 us -> 65 us (0.973)
  Pallas kernels: 65.1 us -> 63.8 us
    pallas_call x1, Pallas kernels: 65.1 us -> 63.8 us  [fast_device(): pl.pallas_call(functools.partial(whole_kernel, size_gx, size_gz, units),...]
where the time goes in v3:
time: 65 us; the launch traced here: 64.8 us
  Pallas kernels  63.8 us (98%)
  local copies, waits for them, and re-layouts  0.97 us (1%)
    pallas_call x1, Pallas kernels, fast_device(): pl.pallas_call(functools.partial(whole_kernel, size_gx, size_gz, units),...  63.8 us

profile of v3, /device:TPU:0, one launch (start us, length us, event | category | flops | bytes accessed | tf_op | source)
XLA Modules:
  0.0 64.8 jit_solution(13787936169038005118)
XLA Ops:
  0.0 63.8 %shard_map.37 = f32[64,32,64]{2,1,0:T(8,128)S(1)} custom-call(f32[64,32,64]{2,1,0:T(8,128)} %bitcast.5, f32[8192,128]{1,0:T(8,128)} %bitcast.4, bf16[3072,256]{1,0:T(8,128)(2,1)} %constant.2.clone.tables_hbm), custom_call_target="tpu_custom_call" | custom-call | tf_op jit(solution)/shard_map/pallas_call | solution.py:505
  63.8 1.0 %copy.5 = f32[64,64,32]{1,2,0:T(8,128)} copy(f32[64,64,32]{1,2,0:T(8,128)S(1)} %bitcast.3) | data formatting | bytes 1048576

commit v4 on v3

--- a/solution.py
+++ b/solution.py
@@ -13,7 +13,7 @@
 LANES = 128
 PARTS = 2
 CHUNKS = 8
-SENT = (3,5,6,7,8,8,8,8,8,8)
+SENT = (3, 5, 6, 7, 8, 8, 8, 8, 8, 8)
 VMEM_BYTES = 61 * 1024 * 1024
 
 
@@ -60,6 +60,11 @@
     return out
 
 
+def unit_order(units):
+    each = units // PARTS
+    return [*range(each)][::-1] + [*range(each, units)]
+
+
 def y_tables(length_y, blocks, units, scale):
     cells = np.arange(length_y // 2)
     freq = np.arange(length_y // 2)
@@ -72,7 +77,7 @@
     back = both * weight[:, None]
 
     def ordered(table):
-        table = table.reshape(blocks, 2, units, 2, -1)[:, :, ::-1]
+        table = table.reshape(blocks, 2, units, 2, -1)[:, :, unit_order(units)]
         table = table.reshape(blocks, 2, PARTS, units // PARTS, 2, -1)
         return table.transpose(1, 2, 0, 3, 4, 5).reshape(2, length_y // 2, -1)
 
@@ -221,22 +226,12 @@
         for a in range(rows):
             remote(raw_own.at[c, a], raw_other.at[c, a], 0, raw_sem.at[c, a], partner).start()
 
-    copies[CHUNKS].wait()
-
-    def extract(step, _):
-        u, m = step // 4, lax.rem(step, 4)
-        for half, out in ((gy, green_own), (1 - gy, green_sent)):
-            at = m * positions + 2 * (half * units + units - 1 - u)
-            out[u, m] = green[pl.ds(at, quarter, stride=4 * positions), :]
-        return 0
-
-    lax.fori_loop(0, 4 * units, extract, 0)
-    for m in range(4):
-        nyquist[m] = green[pl.ds(m * positions + 1, quarter, stride=4 * positions), :]
+    order = unit_order(units)
+
     def green_copy(u, sent=2):
         return remote(green_sent.at[u], green_other.at[u], sent, green_sem.at[u], partner)
 
-    last = units - 1
+    last = order.index(0)
     some = pl.ds(0, quarter // 2 + 8)
     plane_copy = remote(
         green_sent.at[last, :, some], green_other.at[last, :, some], 6, green_sem.at[last], partner
@@ -244,22 +239,32 @@
     distant_copy = remote(nyquist.at[:, some], distant.at[:, some], 3, green_sem.at[units], partner)
     giver = block + (1 - gy) == 0
 
-    for u in range(last):
-        green_copy(u).start()
-
-    @pl.when(giver)
-    def _():
-        distant_copy.start()
-        plane_copy.start()
-
-    @pl.when(jnp.logical_not(giver))
-    def _():
-        green_copy(last, 6).start()
-
-    copies[CHUNKS + 1].wait()
-    transposed(x_tab, x_back)
-    copies[CHUNKS + 2].wait()
-    expand(z_half, z_tab, z_back)
+    def prepare(u):
+        if u == 0:
+            copies[CHUNKS].wait()
+
+        def extract(m, _):
+            for half, out in ((gy, green_own), (1 - gy, green_sent)):
+                at = m * positions + 2 * (half * units + order[u])
+                out[u, m] = green[pl.ds(at, quarter, stride=4 * positions), :]
+            return 0
+
+        lax.fori_loop(0, 4, extract, 0)
+        if u != last:
+            green_copy(u).start()
+            return
+        for m in range(4):
+            nyquist[m] = green[pl.ds(m * positions + 1, quarter, stride=4 * positions), :]
+
+        @pl.when(giver)
+        def _():
+            distant_copy.start()
+            plane_copy.start()
+
+        @pl.when(jnp.logical_not(giver))
+        def _():
+            green_copy(last, 6).start()
+
     copies[CHUNKS + 3].wait()
 
     def transform(c):
@@ -279,6 +284,14 @@
     for c in range(CHUNKS):
         transform(c)
         send_plane(f_sent, f_got, 1, f_sem, 0, c, 1)
+        if c < units:
+            prepare(c)
+        elif c == units:
+            copies[CHUNKS + 1].wait()
+            transposed(x_tab, x_back)
+        elif c == units + 1:
+            copies[CHUNKS + 2].wait()
+            expand(z_half, z_tab, z_back)
     for part in range(1, PARTS):
         send_plane(f_sent, f_got, 1, f_sem, part, 0, CHUNKS)
 
@@ -459,7 +472,7 @@
     moved = f_sent.at[:, pl.ds(0, blocks - 1)]
     remote(moved, moved, 1, f_sem.at[0, 0], partner).wait_send()
     remote(moved, moved, 4, b_sem.at[0, 0], partner).wait_send()
-    most = green_sent.at[pl.ds(0, last)]
+    most = green_sent.at[pl.ds(0, units - 1)]
     remote(most, most, 2, green_sem.at[0], partner).wait_send()
 
     @pl.when(giver)

time: 65 us -> 63.7 us (0.980)
  Pallas kernels: 63.8 us -> 62.6 us
    pallas_call x1, Pallas kernels: 63.8 us -> 62.6 us  [fast_device(): pl.pallas_call(functools.partial(whole_kernel, size_gx, size_gz, units),...]
where the time goes in v4:
time: 63.7 us; the launch traced here: 63.6 us
  Pallas kernels  62.6 us (98%)
  local copies, waits for them, and re-layouts  0.97 us (2%)
    pallas_call x1, Pallas kernels, fast_device(): pl.pallas_call(functools.partial(whole_kernel, size_gx, size_gz, units),...  62.6 us

profile of v4, /device:TPU:0, one launch (start us, length us, event | category | flops | bytes accessed | tf_op | source)
XLA Modules:
  0.0 63.6 jit_solution(17092263439631866922)
XLA Ops:
  0.0 62.6 %shard_map.37 = f32[64,32,64]{2,1,0:T(8,128)S(1)} custom-call(f32[64,32,64]{2,1,0:T(8,128)} %bitcast.5, f32[8192,128]{1,0:T(8,128)} %bitcast.4, bf16[3072,256]{1,0:T(8,128)(2,1)} %constant.2.clone.tables_hbm), custom_call_target="tpu_custom_call" | custom-call | tf_op jit(solution)/shard_map/pallas_call | solution.py:518
  62.6 1.0 %copy.5 = f32[64,64,32]{1,2,0:T(8,128)} copy(f32[64,64,32]{1,2,0:T(8,128)S(1)} %bitcast.3) | data formatting | bytes 1048576

commit v5 on v4

--- a/solution.py
+++ b/solution.py
@@ -318,14 +318,16 @@
         out = jnp.concatenate(out, axis=0)
         return [table_right(out, z_tab[h], z_tab[2 + h]) for h in (gy, 1 - gy)]
 
-    def solve(field, gains_of):
+    def solve(field, own_gain, gain_of):
         freqs = forward(field)
-        for side, gain in enumerate(gains_of()):
+        def weighted(gain, value):
             gain = gain.reshape(4 * quarter, share)
-            spectrum[side] = jnp.concatenate([gain, gain], axis=1) * freqs[side]
-        inverse = sum(
-            table_right(spectrum[side], z_back[h], z_back[2 + h]) for side, h in ((0, gy), (1, 1 - gy))
-        )
+            return jnp.concatenate([gain, gain], axis=1) * value
+
+        spectrum[0] = table_right(weighted(own_gain, freqs[0]), z_back[gy], z_back[2 + gy])
+        spectrum[1] = freqs[1]
+        other = weighted(gain_of(), spectrum[1])
+        inverse = spectrum[0] + table_right(other, z_back[1 - gy], z_back[3 - gy])
         cells = []
         for m in range(4):
             out = inverse[m * quarter : (m + 1) * quarter]
@@ -347,26 +349,27 @@
 
         def gains():
             green_copy(u).wait_recv()
-            return green_own[u], green_other[u]
+            return green_other[u]
 
         def plane_gains():
             plane_copy.wait_recv()
-            return green_own[last], folded(green_other[last])
+            return folded(green_other[last])
 
         def distant_gains():
             distant_copy.wait_recv()
-            return nyquist[...], folded(distant[...])
+            return folded(distant[...])
 
         @pl.when(jnp.logical_not(here))
         def _():
-            lines[c] = solve(lines[c], gains)
+            lines[c] = solve(lines[c], green_own[u], gains)
 
         @pl.when(here)
         def _():
             field = lines[last % each]
             zero = jnp.zeros_like(field)
-            extra[...] = solve(chosen(zero, field), distant_gains)
-            lines[last % each] = chosen(solve(chosen(lines[last % each], zero), plane_gains), extra[...])
+            extra[...] = solve(chosen(zero, field), nyquist[...], distant_gains)
+            again = chosen(lines[last % each], zero)
+            lines[last % each] = chosen(solve(again, green_own[last], plane_gains), extra[...])
 
     def part_step(part, _):
         @pl.when(part == 0)

time: 63.7 us -> 63.7 us (level)
  no operation moved by 1% of the time
where the time goes in v5:
time: 63.7 us; the launch traced here: 63.6 us
  Pallas kernels  62.6 us (98%)
  local copies, waits for them, and re-layouts  0.97 us (2%)
    pallas_call x1, Pallas kernels, fast_device(): pl.pallas_call(functools.partial(whole_kernel, size_gx, size_gz, units),...  62.6 us

profile of v5, /device:TPU:0, one launch (start us, length us, event | category | flops | bytes accessed | tf_op | source)
XLA Modules:
  0.0 63.6 jit_solution(8139504681205130134)
XLA Ops:
  0.0 62.6 %shard_map.37 = f32[64,32,64]{2,1,0:T(8,128)S(1)} custom-call(f32[64,32,64]{2,1,0:T(8,128)} %bitcast.5, f32[8192,128]{1,0:T(8,128)} %bitcast.4, bf16[3072,256]{1,0:T(8,128)(2,1)} %constant.2.clone.tables_hbm), custom_call_target="tpu_custom_call" | custom-call | tf_op jit(solution)/shard_map/pallas_call | solution.py:521
  62.6 1.0 %copy.5 = f32[64,64,32]{1,2,0:T(8,128)} copy(f32[64,64,32]{1,2,0:T(8,128)S(1)} %bitcast.3) | data formatting | bytes 1048576
